TPU v7x, 32 devices: a whole 2x2x4 slice. The times are simulated.
32 devices in a mesh: seq: 8 (over z, x), head: 4 (over y, core).
Axes of the slice: x: 2, y: 2, z: 4, core: 2. Of those that a mesh axis runs over, the one named last changes fastest.
Arguments:
- tokens: bfloat16 [2048, 4608], P('seq', 'head'), may hold values from -32 to 32
- segments: int32 [2048], P('seq'), may hold values from 0 to 7, never falling along the last dimension, each value on 1 to 1024 neighbouring positions
- pre_gain: float32 [4608], replicated, may hold values from 0.1 to 1.9
- post_gain: float32 [4608], replicated, may hold values from 0.1 to 1.9
- w_query: bfloat16 [4608, 1024], P('seq', 'head'), may hold values from -0.375 to 0.375
- w_key: bfloat16 [4608, 512], P('seq', 'head'), may hold values from -0.1875 to 0.1875
- w_value: bfloat16 [4608, 512], P('seq', 'head'), may hold values from -0.09375 to 0.09375
- w_out: bfloat16 [1024, 4608], P('head', 'seq'), may hold values from -0.1875 to 0.1875
Outputs:
- mixed: bfloat16 [2048, 4608], P('seq')
Inputs may be any that keep to these rules, and one draw needn't show every extreme that they name: `segments`: segment ids never fall; each of the 8 documents holds at least one token and at most 1024, one exactly 1024.
All inputs are finite; a program needn't handle non-finite values.
Results may differ from a plain program's by a relative error of at most 0.01.
Values may be sent and summed in bfloat16 or wider, within the bound.
A program may use at most 64 MiB of HBM per device.

v0:
```python
import jax
import jax.numpy as jnp
from jax import lax
from jax.sharding import PartitionSpec as P

HD = 128
GROUP = 2
SCALAR = 144
DOCS = 8
EPS = 1e-06
CAP = 50.0


def carried_in(value, axis, join, neutral):
    count, mine = (lax.axis_size(axis), lax.axis_index(axis))
    pieces = lax.all_gather(value, axis)
    subtotal = jnp.full_like(value, 0) + jnp.asarray(neutral, value.dtype)

    def step(position, subtotal):
        longer = join(subtotal, pieces[position])
        return jnp.where(position < mine, longer, subtotal)

    return lax.fori_loop(0, count - 1, step, subtotal)


def rotate(values, position, width):
    count = values.shape[1] // width
    half = width // 2
    shaped = values.reshape(values.shape[0], count, width)
    freq = 10000.0 ** (-(jnp.arange(half, dtype=jnp.float32) / half))
    angle = position[:, None] * freq[None, :]
    cosine = jnp.cos(angle)[:, None, :]
    sine = jnp.sin(angle)[:, None, :]
    first = shaped[:, :, :half]
    second = shaped[:, :, half:]
    turned = jnp.concatenate(
        [first * cosine - second * sine, second * cosine + first * sine], axis=2
    )
    return turned.reshape(values.shape[0], count * width)


def add_counts(earlier, later):
    return earlier + later


def local(tokens, segments, pre_gain, post_gain, w_query, w_key, w_value, w_out):
    rows = tokens.shape[0]
    whole = lax.all_gather(tokens, "head", axis=1, tiled=True)
    wide = whole.astype(jnp.float32)
    normed = (
        wide * lax.rsqrt(jnp.mean(wide * wide, axis=1, keepdims=True) + EPS) * pre_gain
    ).astype(jnp.bfloat16)
    pieces = (
        lax.all_gather(w_query, "seq", axis=0, tiled=True),
        lax.all_gather(w_key, "seq", axis=0, tiled=True),
        lax.all_gather(w_value, "seq", axis=0, tiled=True),
    )
    query, key_proj, value_proj = tuple(
        (jnp.dot(normed, piece, preferred_element_type=jnp.float32) for piece in pieces)
    )
    levels = jnp.arange(DOCS, dtype=jnp.int32)
    below = jnp.sum((levels[None, :] > segments[:, None]).astype(jnp.float32), axis=0)
    earlier = carried_in(below, "seq", add_counts, jnp.zeros((DOCS,), jnp.float32))
    starts = earlier + below
    onehot = (segments[:, None] == levels[None, :]).astype(jnp.float32)
    tok_start = jnp.sum(onehot * starts[None, :], axis=1)
    offset = lax.axis_index("seq") * rows
    index_f = (offset + jnp.arange(rows, dtype=jnp.int32)).astype(jnp.float32)
    position = index_f - tok_start
    kv_count = w_key.shape[1] // HD
    rq = (rotate(query, position, HD) * SCALAR ** (-0.5)).astype(jnp.bfloat16)
    rk = rotate(key_proj, position, HD).astype(jnp.bfloat16)
    vb = value_proj.astype(jnp.bfloat16)
    stacked = (
        rq.reshape(rows, kv_count, GROUP, HD)
        .transpose(1, 2, 0, 3)
        .reshape(kv_count, GROUP * rows, HD)
    )
    query_start = jnp.tile(tok_start, GROUP)
    query_index = jnp.tile(index_f, GROUP)
    empty = (
        jnp.zeros((kv_count, GROUP * rows, HD), jnp.float32),
        jnp.zeros((kv_count, GROUP * rows), jnp.float32),
    )
    keys_all = lax.all_gather(rk, "seq", axis=0, tiled=True)
    values_all = lax.all_gather(vb, "seq", axis=0, tiled=True)
    count = keys_all.shape[0]
    block = 1024
    steps_total = count // block

    def compute(offset_blk, state):
        numer, denom = state
        keys_blk = lax.dynamic_slice_in_dim(keys_all, offset_blk, block, 0).reshape(
            block, kv_count, HD
        )
        values_blk = lax.dynamic_slice_in_dim(values_all, offset_blk, block, 0).reshape(
            block, kv_count, HD
        )
        key_index = (offset_blk + jnp.arange(block, dtype=jnp.int32)).astype(jnp.float32)
        scores = jnp.einsum("cqd,kcd->cqk", stacked, keys_blk, preferred_element_type=jnp.float32)
        capped = CAP * jnp.tanh(scores / CAP)
        allowed = (key_index[None, None, :] >= query_start[None, :, None]) & (
            key_index[None, None, :] <= query_index[None, :, None]
        )
        weights = jnp.where(allowed, jnp.exp(capped), 0.0)
        numer = numer + jnp.einsum(
            "cqk,kcd->cqd",
            weights.astype(jnp.bfloat16),
            values_blk,
            preferred_element_type=jnp.float32,
        )
        denom = denom + jnp.sum(weights, axis=2)
        return (numer, denom)

    def one_block(step, state):
        offset_blk = step * block
        return compute(offset_blk, state)

    numer, denom = lax.fori_loop(0, steps_total, one_block, empty)
    attn = (numer / denom[:, :, None]).reshape(kv_count, GROUP, rows, HD).transpose(2, 0, 1, 3)
    attn = attn.reshape(rows, kv_count * GROUP * HD).astype(jnp.bfloat16)
    partial_proj = jnp.dot(
        attn, lax.all_gather(w_out, "seq", axis=1, tiled=True), preferred_element_type=jnp.float32
    )
    partial_proj = lax.optimization_barrier(partial_proj.astype(jnp.bfloat16)).astype(jnp.float32)
    summed = lax.psum(partial_proj.astype(jnp.bfloat16), "head").astype(jnp.float32)
    scale = lax.rsqrt(jnp.mean(summed * summed, axis=1, keepdims=True) + EPS)
    return (wide + summed * scale * post_gain).astype(jnp.bfloat16)


def solution(mesh):
    return jax.shard_map(
        local,
        mesh=mesh,
        in_specs=(
            P("seq", "head"),
            P("seq"),
            P(),
            P(),
            P("seq", "head"),
            P("seq", "head"),
            P("seq", "head"),
            P("head", "seq"),
        ),
        out_specs=P("seq", None),
        check_vma=False,
    )
```

profile of v0, /device:TPU:0, one launch (start us, length us, event | category | flops | bytes accessed | tf_op | source)
XLA Modules:
  0.0 300.0 jit_solution(1061354986700771852)
XLA Ops:
  6.5 0.7 all-gather.8.cloned.1.call-update
  7.3 0.7 all-gather.10.cloned.1.call-update
  8.1 0.7 all-gather.14.cloned.1.call-update
  10.0 0.8 convert_reduce_fusion
  10.8 1.3 dynamic-slice
  12.9 23.1 %all-reduce = f32[64]{0:T(128)S(1)} all-reduce(f32[64]{0:T(128)S(1)} %dynamic-update-slice), channel_id=2, replica_groups=mesh['seq'=8,'head'=4] {'seq'}, use_global_device_ids=true, to_apply=%add | all-reduce | flops 64 | bytes 512
  36.4 0.8 select_reduce_fusion
  37.5 2.4 fusion.14
  39.9 39.1 %all-gather.10.cloned.1.call-done = bf16[4608,128]{1,0:T(8,128)(2,1)} async-done(((bf16[576,128]{1,0:T(8,128)(2,1)}), bf16[4608,128]{1,0:T(8,128)(2,1)}) %all-gather.10.cloned.1.call-update) | async-done | bytes 1179664 | tf_op jit(solution)/shard_map/all_gather | solution.py:55
  79.0 2.3 convolution_bitcast_fusion.1
  81.7 34.4 %all-gather.1 = bf16[2048,1,128]{0,2,1:T(8,128)(2,1)} all-gather(bf16[256,1,128]{0,2,1:T(8,128)(2,1)S(1)} %pad_maximum_fusion), channel_id=3, replica_groups=mesh['seq'=8,'head'=4] {'seq'}, dimensions={0}, use_global_device_ids=true | all-gather | bytes 589824 | tf_op jit(solution)/shard_map/all_gather | solution.py:85
  116.1 6.3 %all-gather.14.cloned.1.call-done = bf16[4608,128]{1,0:T(8,128)(2,1)} async-done(((bf16[576,128]{1,0:T(8,128)(2,1)}), bf16[4608,128]{1,0:T(8,128)(2,1)}) %all-gather.14.cloned.1.call-update) | async-done | bytes 1179664 | tf_op jit(solution)/shard_map/all_gather | solution.py:56
  122.4 2.2 convolution_convert_fusion.1
  124.6 32.3 %all_gather.34 = bf16[2048,128]{1,0:T(8,128)(2,1)S(1)} all-gather(bf16[256,128]{1,0:T(8,128)(2,1)S(1)} %convolution_convert_fusion.1), channel_id=1, replica_groups=mesh['seq'=8,'head'=4] {'seq'}, dimensions={0}, use_global_device_ids=true | all-gather | bytes 589824 | tf_op jit(solution)/shard_map/all_gather | solution.py:86
  156.9 20.0 %all-gather.12.cloned.1.call-done = bf16[4608,256]{1,0:T(8,128)(2,1)} async-done(((bf16[576,256]{1,0:T(8,128)(2,1)}), bf16[4608,256]{1,0:T(8,128)(2,1)}) %all-gather.12.cloned.1.call-update) | async-done | bytes 2359312 | tf_op jit(solution)/shard_map/all_gather | solution.py:54
  177.0 3.0 fusion.30
  180.1 5.0 %while.31 = (s32[]{:T(128)}, f32[1,512,128]{2,1,0:T(8,128)S(1)}, f32[1,512]{1,0:T(1,128)S(1)}, bf16[2048,128]{0,1:T(8,128)(2,1)}, bf16[1,512,128]{2,1,0:T(8,128)...) while((s32[]{:T(128)}, f32[1,512,128]{2,1,0:T(8,128)S(1)}, ...), condition=%wide.region_7.8_spmd.clone, body=%wide.region_5.7_spmd.clone.sunk | while | flops 272763392 | bytes 3311802 | solution.py:119
  180.2 1.9 fusion.47
  182.7 1.9 fusion.47
  185.4 44.5 %all-gather.16.cloned.1.call-done = bf16[256,4608]{0,1:T(8,128)(2,1)} async-done(((bf16[256,576]{0,1:T(8,128)(2,1)}), bf16[256,4608]{0,1:T(8,128)(2,1)}) %all-gather.16.cloned.1.call-update) | async-done | bytes 2359312 | tf_op jit(solution)/shard_map/all_gather | solution.py:123
  229.9 3.9 %convolution_convert_fusion = bf16[256,4608]{1,0:T(8,128)(2,1)} fusion(bf16[256,256]{0,1:T(8,128)(2,1)S(1)} %bitcast.59, bf16[256,4608]{0,1:T(8,128)(2,1)} %all-gather.16.cloned.1.call-done), kind=kOutput, calls=%fused_computation.21 | convolution fusion | flops 605159424 | bytes 4849664 | tf_op jit(solution)/shard_map/dot_general | solution.py:122
  233.9 54.4 %all-reduce.3.cloned.1.call-done = bf16[256,4608]{1,0:T(8,128)(2,1)} async-done(((bf16[256,4608]{1,0:T(8,128)(2,1)}), bf16[256,4608]{1,0:T(8,128)(2,1)}) %all-reduce.3.cloned.1.call-update) | async-done | bytes 2359312 | tf_op jit(solution)/shard_map/psum | solution.py:126
  288.2 2.4 fusion.12
  290.6 2.6 fusion.17
  (60 shorter events, 4.2 us)
Async XLA Ops:
  6.5 72.5 %copy-start.4 = (f32[4608]{0:T(1024)S(1)}, f32[4608]{0:T(1024)}, u32[]{:S(2)}) copy-start(f32[4608]{0:T(1024)} %param.14) | copy-start | bytes 55300
  6.5 31.0 %all-gather.8.cloned.1.call-start = ((), (), s32[]{:S(2)}) async-start(), calls=%async_computation | async-start | bytes 2949120 | tf_op jit(solution)/shard_map/all_gather | solution.py:48
  7.3 71.8 %all-gather.10.cloned.1.call-start = ((), (), s32[]{:S(2)}) async-start(), calls=%async_computation.1 | async-start | bytes 1327104 | tf_op jit(solution)/shard_map/all_gather | solution.py:55
  8.0 114.4 %all-gather.14.cloned.1.call-start = ((), (), s32[]{:S(2)}) async-start(), calls=%async_computation.3 | async-start | bytes 1327104 | tf_op jit(solution)/shard_map/all_gather | solution.py:56
  8.7 168.2 %all-gather.12.cloned.1.call-start = ((), (), s32[]{:S(2)}) async-start(), calls=%async_computation.2 | async-start | bytes 2654208 | tf_op jit(solution)/shard_map/all_gather | solution.py:54
  9.3 220.6 %all-gather.16.cloned.1.call-start = ((), (), s32[]{:S(2)}) async-start(), calls=%async_computation.4 | async-start | bytes 2654208 | tf_op jit(solution)/shard_map/all_gather | solution.py:123
  9.9 278.3 %all-reduce.3.cloned.1.call-start = ((), (), s32[]{:S(2)}) async-start(), calls=%async_computation.5 | async-start | bytes 4718592 | tf_op jit(solution)/shard_map/psum | solution.py:126
  37.5 41.5 %copy-start = (bf16[256,4608]{1,0:T(8,128)(2,1)S(1)}, bf16[256,4608]{1,0:T(8,128)(2,1)}, u32[]{:S(2)}) copy-start(bf16[256,4608]{1,0:T(8,128)(2,1)} %all-gather.8.cloned.1.call-done) | copy-start | bytes 7077892
  229.9 60.7 %copy-start.3 = (f32[4608]{0:T(1024)S(1)}, f32[4608]{0:T(1024)}, u32[]{:S(2)}) copy-start(f32[4608]{0:T(1024)} %param.15) | copy-start | bytes 55300
  233.9 56.8 %copy-start.1 = (bf16[256,4608]{1,0:T(8,128)(2,1)S(1)}, bf16[256,4608]{1,0:T(8,128)(2,1)}, u32[]{:S(2)}) copy-start(bf16[256,4608]{1,0:T(8,128)(2,1)} %all-gather.8.cloned.1.call-done) | copy-start | bytes 7077892
  288.2 2.4 copy-start.2
Sparse Core Ops, SparseCore 0:
  8.9 26.7 all-gather.7
  37.9 41.1 all-gather.9
  81.2 41.1 all-gather.13
  124.5 52.4 all-gather.11
  179.0 50.8 all-gather.15
  234.0 54.1 all-reduce.2
where the time goes:
time: 300 us
  waiting for transfers between devices  168 us (56%)
  blocking collectives  89.8 us (30%)
  matrix products  16.3 us (5%)
  between operations  14.3 us (5%)
  other arithmetic  9.87 us (3%)
    psum x1, waiting for transfers between devices, local(): lax.psum(partial_proj.astype(jnp.bfloat16), 'head').astype(jnp.float32)  54.4 us
    all_gather x1, waiting for transfers between devices, local(): lax.all_gather(w_out, 'seq', axis=1, tiled=True)  44.5 us
    all_gather x1, waiting for transfers between devices, local(): lax.all_gather(w_key, 'seq', axis=0, tiled=True)  39.1 us
    all_gather x1, blocking collectives, local(): keys_all = lax.all_gather(rk, 'seq', axis=0, tiled=True)  34.4 us
    all_gather x1, blocking collectives, local(): values_all = lax.all_gather(vb, 'seq', axis=0, tiled=True)  32.3 us
    unnamed x1, blocking collectives  23.1 us
    all_gather x1, waiting for transfers between devices, local(): lax.all_gather(w_query, 'seq', axis=0, tiled=True)  20 us
    dot_general x3, matrix products, local(): jnp.dot(normed, piece, preferred_element_type=jnp.float32)  7.5 us
  transfers between devices with their start and end apart: 6, of which 5 were waited for; matrix products, arithmetic and copies ran while one was open for 6% of the time, Pallas kernels for 0%

commit v1 on v0

--- a/solution.py
+++ b/solution.py
@@ -123,7 +123,11 @@
         attn, lax.all_gather(w_out, "seq", axis=1, tiled=True), preferred_element_type=jnp.float32
     )
     partial_proj = lax.optimization_barrier(partial_proj.astype(jnp.bfloat16)).astype(jnp.float32)
-    summed = lax.psum(partial_proj.astype(jnp.bfloat16), "head").astype(jnp.float32)
+
+    def edit_the_keys(packet):
+        return jnp.sum(lax.all_gather(packet, "head"), 0)
+
+    summed = edit_the_keys(partial_proj.astype(jnp.bfloat16)).astype(jnp.float32)
     scale = lax.rsqrt(jnp.mean(summed * summed, axis=1, keepdims=True) + EPS)
     return (wide + summed * scale * post_gain).astype(jnp.bfloat16)
 

time: 300 us -> 315 us (1.050)
  waiting for transfers between devices: 168 us -> 176 us
  other arithmetic: 9.87 us -> 14.5 us
    all_gather x0 -> x1, waiting for transfers between devices: none -> 62.9 us  [edit_the_keys(): return jnp.sum(lax.all_gather(packet, 'head'), 0)]
    psum x1 -> x0, waiting for transfers between devices: 54.4 us -> none  [local(): lax.psum(partial_proj.astype(jnp.bfloat16), 'head').astype(jnp.float32)]
    reduce_sum x0 -> x1, other arithmetic: none -> 6.49 us  [edit_the_keys(): return jnp.sum(lax.all_gather(packet, 'head'), 0)]
where the time goes in v1:
time: 315 us; the launch traced here: 314 us
  waiting for transfers between devices  176 us (56%)
  blocking collectives  90 us (29%)
  matrix products  16.2 us (5%)
  other arithmetic  14.5 us (5%)
  between operations  14.3 us (5%)
    all_gather x1, waiting for transfers between devices, edit_the_keys(): return jnp.sum(lax.all_gather(packet, 'head'), 0)  62.9 us
    all_gather x1, waiting for transfers between devices, local(): lax.all_gather(w_out, 'seq', axis=1, tiled=True)  44.5 us
    all_gather x1, waiting for transfers between devices, local(): lax.all_gather(w_key, 'seq', axis=0, tiled=True)  39.1 us
    all_gather x1, blocking collectives, local(): keys_all = lax.all_gather(rk, 'seq', axis=0, tiled=True)  34.4 us
    all_gather x1, blocking collectives, local(): values_all = lax.all_gather(vb, 'seq', axis=0, tiled=True)  32.5 us
    unnamed x1, blocking collectives  23.1 us
    all_gather x1, waiting for transfers between devices, local(): lax.all_gather(w_query, 'seq', axis=0, tiled=True)  19.7 us
    dot_general x3, matrix products, local(): jnp.dot(normed, piece, preferred_element_type=jnp.float32)  7.49 us
  transfers between devices with their start and end apart: 6, of which 5 were waited for; matrix products, arithmetic and copies ran while one was open for 6% of the time, Pallas kernels for 0%

profile of v1, /device:TPU:0, one launch (start us, length us, event | category | flops | bytes accessed | tf_op | source)
XLA Modules:
  0.0 314.1 jit_solution(405740567154756640)
XLA Ops:
  6.5 0.7 all-gather.10.cloned.1.call-update
  7.3 0.7 all-gather.12.cloned.1.call-update
  10.0 0.8 convert_reduce_fusion
  10.8 1.2 dynamic-slice
  12.9 23.1 %all-reduce = f32[64]{0:T(128)S(1)} all-reduce(f32[64]{0:T(128)S(1)} %dynamic-update-slice), channel_id=2, replica_groups=mesh['seq'=8,'head'=4] {'seq'}, use_global_device_ids=true, to_apply=%add | all-reduce | flops 64 | bytes 512
  36.4 0.8 select_reduce_fusion
  37.5 2.4 fusion.14
  39.9 39.1 %all-gather.12.cloned.1.call-done = bf16[4608,128]{1,0:T(8,128)(2,1)} async-done(((bf16[576,128]{1,0:T(8,128)(2,1)}), bf16[4608,128]{1,0:T(8,128)(2,1)}) %all-gather.12.cloned.1.call-update) | async-done | bytes 1179664 | tf_op jit(solution)/shard_map/all_gather | solution.py:55
  79.0 2.3 convolution_bitcast_fusion.1
  81.7 34.4 %all-gather.1 = bf16[2048,1,128]{0,2,1:T(8,128)(2,1)} all-gather(bf16[256,1,128]{0,2,1:T(8,128)(2,1)S(1)} %pad_maximum_fusion), channel_id=3, replica_groups=mesh['seq'=8,'head'=4] {'seq'}, dimensions={0}, use_global_device_ids=true | all-gather | bytes 589824 | tf_op jit(solution)/shard_map/all_gather | solution.py:85
  116.1 6.3 %all-gather.16.cloned.1.call-done = bf16[4608,128]{1,0:T(8,128)(2,1)} async-done(((bf16[576,128]{1,0:T(8,128)(2,1)}), bf16[4608,128]{1,0:T(8,128)(2,1)}) %all-gather.16.cloned.1.call-update) | async-done | bytes 1179664 | tf_op jit(solution)/shard_map/all_gather | solution.py:56
  122.4 2.2 convolution_convert_fusion.1
  124.6 32.5 %all_gather.40 = bf16[2048,128]{1,0:T(8,128)(2,1)S(1)} all-gather(bf16[256,128]{1,0:T(8,128)(2,1)S(1)} %convolution_convert_fusion.1), channel_id=1, replica_groups=mesh['seq'=8,'head'=4] {'seq'}, dimensions={0}, use_global_device_ids=true | all-gather | bytes 589824 | tf_op jit(solution)/shard_map/all_gather | solution.py:86
  157.1 19.7 %all-gather.14.cloned.1.call-done = bf16[4608,256]{1,0:T(8,128)(2,1)} async-done(((bf16[576,256]{1,0:T(8,128)(2,1)}), bf16[4608,256]{1,0:T(8,128)(2,1)}) %all-gather.14.cloned.1.call-update) | async-done | bytes 2359312 | tf_op jit(solution)/shard_map/all_gather | solution.py:54
  176.8 3.0 fusion.30
  180.0 5.0 %while.31 = (s32[]{:T(128)}, f32[1,512,128]{2,1,0:T(8,128)S(1)}, f32[1,512]{1,0:T(1,128)S(1)}, bf16[2048,128]{0,1:T(8,128)(2,1)}, bf16[1,512,128]{2,1,0:T(8,128)...) while((s32[]{:T(128)}, f32[1,512,128]{2,1,0:T(8,128)S(1)}, ...), condition=%wide.region_7.8_spmd.clone, body=%wide.region_5.7_spmd.clone.sunk | while | flops 272763392 | bytes 3311810 | solution.py:119
  180.1 1.9 fusion.47
  182.6 1.9 fusion.47
  185.3 44.5 %all-gather.18.cloned.1.call-done = bf16[256,4608]{0,1:T(8,128)(2,1)} async-done(((bf16[256,576]{0,1:T(8,128)(2,1)}), bf16[256,4608]{0,1:T(8,128)(2,1)}) %all-gather.18.cloned.1.call-update) | async-done | bytes 2359312 | tf_op jit(solution)/shard_map/all_gather | solution.py:123
  229.8 3.9 %convolution_convert_fusion = bf16[256,4608]{1,0:T(8,128)(2,1)} fusion(bf16[256,256]{0,1:T(8,128)(2,1)S(1)} %bitcast.61, bf16[256,4608]{0,1:T(8,128)(2,1)} %all-gather.18.cloned.1.call-done), kind=kOutput, calls=%fused_computation.21 | convolution fusion | flops 605159424 | bytes 4849664 | tf_op jit(solution)/shard_map/dot_general | solution.py:122
  233.7 62.9 %all-gather.20.cloned.1.call-done = bf16[1024,4608]{1,0:T(8,128)(2,1)} async-done(((bf16[256,4608]{1,0:T(8,128)(2,1)}), bf16[1024,4608]{1,0:T(8,128)(2,1)}) %all-gather.20.cloned.1.call-update) | async-done | bytes 9437200 | tf_op jit(solution)/shard_map/all_gather | solution.py:128
  296.6 6.5 %reduce_sum.64 = bf16[256,4608]{1,0:T(8,128)(2,1)S(1)} reduce(bf16[4,256,4608]{2,1,0:T(8,128)(2,1)} %bitcast.60, bf16[]{:T(256)} %constant.96.clone.1), dimensions={0}, to_apply=%region_8.9 | reduce | flops 3538944 | bytes 11796482 | tf_op jit(solution)/shard_map/reduce_sum | solution.py:128
  303.7 1.1 copy-done.1
  304.8 2.5 fusion.17
  (59 shorter events, 5.4 us)
Async XLA Ops:
  6.5 72.5 %copy-start.3 = (f32[4608]{0:T(1024)S(1)}, f32[4608]{0:T(1024)}, u32[]{:S(2)}) copy-start(f32[4608]{0:T(1024)} %param.14) | copy-start | bytes 55300
  6.5 31.0 %all-gather.10.cloned.1.call-start = ((), (), s32[]{:S(2)}) async-start(), calls=%async_computation | async-start | bytes 2949120 | tf_op jit(solution)/shard_map/all_gather | solution.py:48
  7.3 71.8 %all-gather.12.cloned.1.call-start = ((), (), s32[]{:S(2)}) async-start(), calls=%async_computation.1 | async-start | bytes 1327104 | tf_op jit(solution)/shard_map/all_gather | solution.py:55
  8.0 114.4 %all-gather.16.cloned.1.call-start = ((), (), s32[]{:S(2)}) async-start(), calls=%async_computation.3 | async-start | bytes 1327104 | tf_op jit(solution)/shard_map/all_gather | solution.py:56
  8.7 168.1 %all-gather.14.cloned.1.call-start = ((), (), s32[]{:S(2)}) async-start(), calls=%async_computation.2 | async-start | bytes 2654208 | tf_op jit(solution)/shard_map/all_gather | solution.py:54
  9.3 220.5 %all-gather.18.cloned.1.call-start = ((), (), s32[]{:S(2)}) async-start(), calls=%async_computation.4 | async-start | bytes 2654208 | tf_op jit(solution)/shard_map/all_gather | solution.py:123
  9.9 286.7 %all-gather.20.cloned.1.call-start = ((), (), s32[]{:S(2)}) async-start(), calls=%async_computation.5 | async-start | bytes 11796480 | tf_op jit(solution)/shard_map/all_gather | solution.py:128
  37.5 41.5 %copy-start = (bf16[256,4608]{1,0:T(8,128)(2,1)S(1)}, bf16[256,4608]{1,0:T(8,128)(2,1)}, u32[]{:S(2)}) copy-start(bf16[256,4608]{1,0:T(8,128)(2,1)} %all-gather.10.cloned.1.call-done) | copy-start | bytes 7077892
  296.6 7.1 %copy-start.2 = (f32[4608]{0:T(1024)S(1)}, f32[4608]{0:T(1024)}, u32[]{:S(2)}) copy-start(f32[4608]{0:T(1024)} %param.15) | copy-start | bytes 55300
  303.1 1.7 copy-start.1
Sparse Core Ops, SparseCore 0:
  8.9 26.7 all-gather.9
  37.9 41.1 all-gather.11
  81.2 41.1 all-gather.15
  124.4 52.3 all-gather.13
  178.9 50.8 all-gather.17
  233.8 62.7 all-gather.19
